TPU v7x, 128 devices: a whole 4x4x4 slice. The times are simulated.
128 devices in a mesh: data: 4 (over z), col: 4 (over y), row: 8 (over x, core).
Axes of the slice: x: 4, y: 4, z: 4, core: 2. Of those that a mesh axis runs over, the one named last changes fastest.
Arguments:
- x_in: bfloat16 [4096, 3072], P(None, 'row')
- h_act: bfloat16 [4096, 8192], P(None, 'row')
- d_gate: bfloat16 [4096, 8192], P(None, 'col')
- d_up: bfloat16 [4096, 8192], P(None, 'col')
- d_out: bfloat16 [4096, 3072], P(None, 'col')
- w_gate: float32 [3072, 8192], P('row', 'col')
- w_up: float32 [3072, 8192], P('row', 'col')
- w_down: float32 [8192, 3072], P('row', 'col')
- r_gate: float32 [3072], P('row')
- c_gate: float32 [8192], P('col')
- r_up: float32 [3072], P('row')
- c_up: float32 [8192], P('col')
- r_down: float32 [8192], P('row')
- c_down: float32 [3072], P('col')
- beta_two: float32 [], replicated
- rel_step: float32 [], replicated
- clip_thr: float32 [], replicated
Outputs:
- output 1: float32 [3072, 8192], P('row', 'col')
- output 2: float32 [3072, 8192], P('row', 'col')
- output 3: float32 [8192, 3072], P('row', 'col')
- output 4: float32 [3072], P('row')
- output 5: float32 [8192], P('col')
- output 6: float32 [3072], P('row')
- output 7: float32 [8192], P('col')
- output 8: float32 [8192], P('row')
- output 9: float32 [3072], P('col')
All inputs are finite; a program needn't handle non-finite values.
Results may differ from a plain program's by a relative error of at most 0.001.
Values are sent between devices in bfloat16 or wider.
A program may use at most 1 GiB of HBM per device.

v0:
```python
import jax
import jax.numpy as jnp
from jax import lax
from jax.sharding import PartitionSpec as P

EPS_SQ = 1e-30
EPS_SCALE = 1e-3
CONTRACT_TOKENS = (((0,), (0,)), ((), ()))


def solution(mesh):
    row_count = mesh.shape["row"]
    col_count = mesh.shape["col"]

    def block_step(w_blk, act_in, cot_out, r_old, c_old, beta_two, rel_step, clip_thr):
        g_blk = lax.dot_general(act_in, cot_out, CONTRACT_TOKENS, preferred_element_type=jnp.float32)
        m_total = g_blk.shape[0] * row_count
        n_total = g_blk.shape[1] * col_count
        q_blk = g_blk * g_blk + EPS_SQ
        row_sum = lax.psum(jnp.sum(q_blk, axis=1), "col")
        col_sum = lax.psum(jnp.sum(q_blk, axis=0), "row")
        r_new = beta_two * r_old + (1.0 - beta_two) * (row_sum / n_total)
        c_new = beta_two * c_old + (1.0 - beta_two) * (col_sum / m_total)
        r_mean = lax.psum(jnp.sum(r_new), "row") / m_total
        u_blk = g_blk / jnp.sqrt(r_new[:, None] * c_new[None, :] / r_mean)
        u_rms = jnp.sqrt(lax.psum(jnp.sum(u_blk * u_blk), ("row", "col")) / (m_total * n_total))
        w_rms = jnp.sqrt(lax.psum(jnp.sum(w_blk * w_blk), ("row", "col")) / (m_total * n_total))
        u_hat = u_blk / jnp.maximum(1.0, u_rms / clip_thr)
        step_size = rel_step * jnp.maximum(EPS_SCALE, w_rms)
        return w_blk - step_size * u_hat, r_new, c_new

    def local_program(x_in, h_act, d_gate, d_up, d_out, w_gate, w_up, w_down, r_gate, c_gate, r_up, c_up, r_down, c_down, beta_two, rel_step, clip_thr):
        gate_out = block_step(w_gate, x_in, d_gate, r_gate, c_gate, beta_two, rel_step, clip_thr)
        up_out = block_step(w_up, x_in, d_up, r_up, c_up, beta_two, rel_step, clip_thr)
        down_out = block_step(w_down, h_act, d_out, r_down, c_down, beta_two, rel_step, clip_thr)
        return (gate_out[0], up_out[0], down_out[0], gate_out[1], gate_out[2], up_out[1], up_out[2], down_out[1], down_out[2])

    act_spec = P(None, "row")
    cot_spec = P(None, "col")
    w_spec = P("row", "col")
    r_spec = P("row")
    c_spec = P("col")
    s_spec = P()
    return jax.shard_map(local_program, mesh=mesh, in_specs=(act_spec, act_spec, cot_spec, cot_spec, cot_spec, w_spec, w_spec, w_spec, r_spec, c_spec, r_spec, c_spec, r_spec, c_spec, s_spec, s_spec, s_spec), out_specs=(w_spec, w_spec, w_spec, r_spec, c_spec, r_spec, c_spec, r_spec, c_spec), check_vma=False)
```

profile of v0, /device:TPU:72, one launch (start us, length us, event | category | flops | bytes accessed | tf_op | source)
XLA Modules:
  0.0 167.6 jit_solution(14219552141248803665)
XLA Ops:
  0.6 0.0 copy-start
  2.9 0.0 copy-start.7
  2.9 3.5 %multiply_reduce_fusion.1 = f32[]{:T(128)} fusion(f32[1024,768]{1,0:T(8,128)} %param.24), kind=kLoop, calls=%fused_computation.4 | loop fusion | flops 1572863 | bytes 3145732 | tf_op jit(solution)/shard_map/reduce_sum | solution.py:27
  6.5 3.5 %multiply_reduce_fusion.3 = (f32[]{:T(128)}, f32[]{:T(128)}) fusion(f32[384,2048]{1,0:T(8,128)} %param.23, f32[384,2048]{1,0:T(8,128)S(1)} %copy-done.7), kind=kLoop, calls=%fused_computation.9 | loop fusion | flops 3145726 | bytes 6291464 | tf_op jit(solution)/shard_map/reduce_sum | solution.py:27
  9.9 10.7 %fusion.4 = (f32[768]{0:T(1024)S(1)}, f32[1024]{0:T(1024)S(1)}, f32[1024,768]{1,0:T(8,128)}) fusion(bf16[4096,1024]{1,0:T(8,128)(2,1)} %param.18, bf16[4096,768]{1,0:T(8,128)(2,1)S(1)} %copy-done.22), kind=kOutput, calls=%fused_computation.19 | convolution fusion | flops 6445594624 | bytes 17832960 | tf_op jit(solution)/shard_map/dot_general | solution.py:16
  20.6 0.0 slice-done.1
  20.6 9.1 %fusion = (f32[2048]{0:T(1024)S(1)}, f32[384]{0:T(512)S(1)}, f32[384,2048]{1,0:T(8,128)}) fusion(bf16[4096,384]{1,0:T(8,128)(2,1)S(1)} %copy-done, bf16[4096,2048]{1,0:T(8,128)(2,1)S(1)} %bitcast.7), kind=kOutput, calls=%fused_computation.15 | convolution fusion | flops 6445594112 | bytes 23078400 | tf_op jit(solution)/shard_map/dot_general | solution.py:16
  29.7 11.5 %fusion.2 = (f32[2048]{0:T(1024)S(1)}, f32[384]{0:T(512)S(1)}, f32[384,2048]{1,0:T(8,128)}) fusion(bf16[4096,384]{1,0:T(8,128)(2,1)S(1)} %copy-done, bf16[4096,2048]{1,0:T(8,128)(2,1)} %param.20), kind=kOutput, calls=%fused_computation.17 | convolution fusion | flops 6445594112 | bytes 23078400 | tf_op jit(solution)/shard_map/dot_general | solution.py:16
  41.2 9.1 %all-reduce.2 = (f32[384]{0:T(512)S(1)}, f32[384]{0:T(512)S(1)}, f32[1024]{0:T(1024)S(1)}) all-reduce(f32[384]{0:T(512)S(1)} %get-tuple-element.14, f32[384]{0:T(512)S(1)} %get-tuple-element.12, f32[1024]{0:T(1024)S(1)} %get-tuple-element.10), channel_id=1, replica_groups=mesh['data'=4,'col'=4,'row'=8] {'col'}, use_global_device_ids=true, to_apply=%region_3.0 | all-reduce | flops 1792 | bytes 14336 | tf_op jit(solution)/shard_map/psum | solution.py:20
  50.3 0.6 fusion.7
  50.9 0.0 copy-done.18
  50.9 0.6 fusion.6
  51.5 24.8 %all-reduce.1 = (f32[]{:T(128)}, f32[2048]{0:T(1024)S(1)}, f32[]{:T(128)}, f32[2048]{0:T(1024)S(1)}, f32[]{:T(128)}, /*index=5*/f32[768]{0:T(1024)S(1)}) all-reduce(f32[]{:T(128)} %get-tuple-element.39, f32[2048]{0:T(1024)S(1)} %get-tuple-element.13, f32[]{:T(128)} %get-tuple-element.32, ...), channel_id=1, replica_groups=mesh['data'=4,'col'=4,'row'=8] {'row'}, use_global_device_ids=true, to_apply=%region_7.0 | all-reduce | flops 4867 | bytes 38936 | tf_op jit(solution)/shard_map/psum | solution.py:24
  78.3 0.0 copy-start.10
  78.3 0.0 copy-start.17
  78.4 0.0 copy-start.5
  78.4 3.6 %multiply_reduce_fusion.4 = f32[]{:T(128)} fusion(f32[384,2048]{1,0:T(8,128)} %get-tuple-element.36, f32[]{:T(128)S(6)} %div.90, f32[2048]{0:T(1024)S(1)} %multiply_add_fusion.4, f32[384]{0:T(512)S(1)} %get-tuple-element.40), kind=kLoop, calls=%fused_computation.11 | loop fusion | flops 3932159 | bytes 3155464 | tf_op jit(solution)/shard_map/reduce_sum | solution.py:26
  82.0 0.0 copy-done.2
  82.0 0.0 copy-start.13
  82.0 2.0 %multiply_reduce_fusion = f32[]{:T(128)} fusion(f32[1024,768]{1,0:T(8,128)S(1)} %copy-done.2, f32[]{:T(128)S(6)} %div.108, f32[768]{0:T(1024)S(1)} %multiply_add_fusion.5, f32[1024]{0:T(1024)S(1)} %get-tuple-element.31), kind=kLoop, calls=%fused_computation.1 | loop fusion | flops 3932159 | bytes 3152904 | tf_op jit(solution)/shard_map/reduce_sum | solution.py:26
  84.0 0.0 copy-start.11
  84.0 1.9 %multiply_reduce_fusion.2 = f32[]{:T(128)} fusion(f32[384,2048]{1,0:T(8,128)S(1)} %copy-done.5, f32[]{:T(128)S(6)} %div.99, f32[2048]{0:T(1024)S(1)} %multiply_add_fusion.3, f32[384]{0:T(512)S(1)} %get-tuple-element.33), kind=kLoop, calls=%fused_computation.6 | loop fusion | flops 3932159 | bytes 3155464 | tf_op jit(solution)/shard_map/reduce_sum | solution.py:26
  85.9 66.2 %all-reduce = (f32[]{:T(128)}, f32[]{:T(128)}, f32[]{:T(128)}, f32[]{:T(128)}, f32[]{:T(128)}, /*index=5*/f32[]{:T(128)}) all-reduce(f32[]{:T(128)} %multiply_reduce_fusion.4, f32[]{:T(128)} %get-tuple-element.42, f32[]{:T(128)} %multiply_reduce_fusion.2, ...), channel_id=1, replica_groups=mesh['data'=4,'col'=4,'row'=8] {'row','col'}, use_global_device_ids=true, to_apply=%region_9.0 | all-reduce | flops 6 | bytes 48 | tf_op jit(solution)/shard_map/psum | solution.py:26
  156.3 0.0 copy-start.6
  156.3 0.0 copy-start.8
  156.3 4.9 %multiply_subtract_fusion.2 = f32[384,2048]{1,0:T(8,128)} fusion(f32[384,2048]{1,0:T(8,128)} %param.22, f32[]{:T(128)S(6)} %max.19, f32[]{:T(128)S(6)} %mul.162, f32[384,2048]{1,0:T(8,128)S(1)} %copy-done.4, f32[]{:T(128)S(6)} %div.90, f32[2048]{0:T(1024)S(1)} %multiply_add_fusion.4, f32[384]{0:T(512)S(1)} %get-tuple-element.40), kind=kLoop, calls=%fused_computation.10 | loop fusion | flops 4718592 | bytes 9446924 | tf_op jit(solution)/shard_map/sub | solution.py:30
  161.2 0.0 copy-start.9
  161.2 0.0 copy-start.1
  161.2 2.6 %multiply_subtract_fusion.1 = f32[384,2048]{1,0:T(8,128)} fusion(f32[384,2048]{1,0:T(8,128)S(1)} %copy-done.8, f32[]{:T(128)S(6)} %max.21, f32[]{:T(128)S(6)} %mul.181, f32[384,2048]{1,0:T(8,128)S(1)} %copy-done.6, f32[]{:T(128)S(6)} %div.99, f32[2048]{0:T(1024)S(1)} %multiply_add_fusion.3, f32[384]{0:T(512)S(1)} %get-tuple-element.33), kind=kLoop, calls=%fused_computation.5 | loop fusion | flops 4718592 | bytes 9446924 | tf_op jit(solution)/shard_map/sub | solution.py:30
  163.8 0.0 copy-done.12
  163.8 1.3 copy-done.9
  165.2 2.5 %multiply_subtract_fusion = f32[1024,768]{1,0:T(8,128)} fusion(f32[1024,768]{1,0:T(8,128)S(1)} %copy-done.9, f32[]{:T(128)S(6)} %max.23, f32[]{:T(128)S(6)} %mul.194, f32[1024,768]{1,0:T(8,128)S(1)} %copy-done.3, f32[]{:T(128)S(6)} %div.108, f32[768]{0:T(1024)S(1)} %multiply_add_fusion.5, f32[1024]{0:T(1024)S(1)} %get-tuple-element.31), kind=kLoop, calls=%fused_computation | loop fusion | flops 4718592 | bytes 9444364 | tf_op jit(solution)/shard_map/sub | solution.py:30
  (42 shorter events, 0.1 us)
Async XLA Ops:
  0.6 20.0 %copy-start = (bf16[4096,384]{1,0:T(8,128)(2,1)S(1)}, bf16[4096,384]{1,0:T(8,128)(2,1)}, u32[]{:S(2)}) copy-start(bf16[4096,384]{1,0:T(8,128)(2,1)} %param.17) | copy-start | bytes 9437188
  2.9 3.5 %copy-start.7 = (f32[384,2048]{1,0:T(8,128)S(1)}, f32[384,2048]{1,0:T(8,128)}, u32[]{:S(2)}) copy-start(f32[384,2048]{1,0:T(8,128)} %param.22) | copy-start | bytes 9437188
  2.9 7.0 %copy-start.22 = (bf16[4096,768]{1,0:T(8,128)(2,1)S(1)}, bf16[4096,768]{1,0:T(8,128)(2,1)}, u32[]{:S(2)}) copy-start(bf16[4096,768]{1,0:T(8,128)(2,1)} %param.21) | copy-start | bytes 18874372
  6.4 14.1 %slice-start = ((s8[16777216]{0:T(1024)(128)(4,1)}), s8[4194304]{0:T(1024)(128)(4,1)S(1)}, s32[]{:S(2)}) async-start(s8[16777216]{0:T(1024)(128)(4,1)} %bitcast.6), calls=%async_computation | async-start | bytes 8388608
  9.9 10.7 %slice-start.1 = ((s8[16777216]{0:T(1024)(128)(4,1)}), s8[4194304]{0:T(1024)(128)(4,1)S(1)}, s32[]{:S(2)}) async-start(s8[16777216]{0:T(1024)(128)(4,1)} %bitcast.6), calls=%async_computation.1 | async-start | bytes 8388608
  9.9 10.7 %slice-start.2 = ((s8[16777216]{0:T(1024)(128)(4,1)}), s8[4194304]{0:T(1024)(128)(4,1)S(1)}, s32[]{:S(2)}) async-start(s8[16777216]{0:T(1024)(128)(4,1)} %bitcast.6), calls=%async_computation.2 | async-start | bytes 8388608
  9.9 10.7 %slice-start.3 = ((s8[16777216]{0:T(1024)(128)(4,1)}), s8[4194304]{0:T(1024)(128)(4,1)S(1)}, s32[]{:S(2)}) async-start(s8[16777216]{0:T(1024)(128)(4,1)} %bitcast.6), calls=%async_computation.3 | async-start | bytes 8388608
  29.7 20.6 %copy-start.20 = (f32[384]{0:T(512)S(1)}, f32[384]{0:T(512)}, u32[]{:S(2)}) copy-start(f32[384]{0:T(512)} %param.27) | copy-start | bytes 4612
  29.7 20.6 %copy-start.21 = (f32[384]{0:T(512)S(1)}, f32[384]{0:T(512)}, u32[]{:S(2)}) copy-start(f32[384]{0:T(512)} %param.25) | copy-start | bytes 4612
  29.7 21.2 %copy-start.18 = (f32[1024]{0:T(1024)S(1)}, f32[1024]{0:T(1024)}, u32[]{:S(2)}) copy-start(f32[1024]{0:T(1024)} %param.29) | copy-start | bytes 12292
  29.7 48.6 %copy-start.16 = (f32[2048]{0:T(1024)S(1)}, f32[2048]{0:T(1024)}, u32[]{:S(2)}) copy-start(f32[2048]{0:T(1024)} %param.26) | copy-start | bytes 24580
  41.2 40.7 %copy-start.19 = (f32[768]{0:T(1024)S(1)}, f32[768]{0:T(1024)}, u32[]{:S(2)}) copy-start(f32[768]{0:T(1024)} %param.30) | copy-start | bytes 9220
  41.2 40.7 %copy-start.2 = (f32[1024,768]{1,0:T(8,128)S(1)}, f32[1024,768]{1,0:T(8,128)}, u32[]{:S(2)}) copy-start(f32[1024,768]{1,0:T(8,128)} %get-tuple-element.38) | copy-start | bytes 9437188
  50.9 105.3 %copy-start.15 = (f32[384]{0:T(512)}, f32[384]{0:T(512)S(1)}, u32[]{:S(2)}) copy-start(f32[384]{0:T(512)S(1)} %get-tuple-element.40) | copy-start | bytes 4612
  50.9 110.2 %copy-start.14 = (f32[384]{0:T(512)}, f32[384]{0:T(512)S(1)}, u32[]{:S(2)}) copy-start(f32[384]{0:T(512)S(1)} %get-tuple-element.33) | copy-start | bytes 4612
  51.5 112.3 %copy-start.12 = (f32[1024]{0:T(1024)}, f32[1024]{0:T(1024)S(1)}, u32[]{:S(2)}) copy-start(f32[1024]{0:T(1024)S(1)} %get-tuple-element.31) | copy-start | bytes 12292
  78.3 77.9 %copy-start.10 = (f32[2048]{0:T(1024)}, f32[2048]{0:T(1024)S(1)}, u32[]{:S(2)}) copy-start(f32[2048]{0:T(1024)S(1)} %multiply_add_fusion.4) | copy-start | bytes 24580
  78.3 5.6 %copy-start.17 = (f32[2048]{0:T(1024)S(1)}, f32[2048]{0:T(1024)}, u32[]{:S(2)}) copy-start(f32[2048]{0:T(1024)} %param.28) | copy-start | bytes 24580
  78.4 5.6 %copy-start.5 = (f32[384,2048]{1,0:T(8,128)S(1)}, f32[384,2048]{1,0:T(8,128)}, u32[]{:S(2)}) copy-start(f32[384,2048]{1,0:T(8,128)} %get-tuple-element.37) | copy-start | bytes 9437188
  82.0 81.9 %copy-start.13 = (f32[768]{0:T(1024)}, f32[768]{0:T(1024)S(1)}, u32[]{:S(2)}) copy-start(f32[768]{0:T(1024)S(1)} %multiply_add_fusion.5) | copy-start | bytes 9220
  84.0 72.3 %copy-start.4 = (f32[384,2048]{1,0:T(8,128)S(1)}, f32[384,2048]{1,0:T(8,128)}, u32[]{:S(2)}) copy-start(f32[384,2048]{1,0:T(8,128)} %get-tuple-element.36) | copy-start | bytes 9437188
  84.0 77.2 %copy-start.11 = (f32[2048]{0:T(1024)}, f32[2048]{0:T(1024)S(1)}, u32[]{:S(2)}) copy-start(f32[2048]{0:T(1024)S(1)} %multiply_add_fusion.3) | copy-start | bytes 24580
  156.3 4.9 %copy-start.6 = (f32[384,2048]{1,0:T(8,128)S(1)}, f32[384,2048]{1,0:T(8,128)}, u32[]{:S(2)}) copy-start(f32[384,2048]{1,0:T(8,128)} %get-tuple-element.37) | copy-start | bytes 9437188
  156.3 4.9 %copy-start.8 = (f32[384,2048]{1,0:T(8,128)S(1)}, f32[384,2048]{1,0:T(8,128)}, u32[]{:S(2)}) copy-start(f32[384,2048]{1,0:T(8,128)} %param.23) | copy-start | bytes 9437188
  161.2 2.7 %copy-start.3 = (f32[1024,768]{1,0:T(8,128)S(1)}, f32[1024,768]{1,0:T(8,128)}, u32[]{:S(2)}) copy-start(f32[1024,768]{1,0:T(8,128)} %get-tuple-element.38) | copy-start | bytes 9437188
  161.2 4.0 %copy-start.9 = (f32[1024,768]{1,0:T(8,128)S(1)}, f32[1024,768]{1,0:T(8,128)}, u32[]{:S(2)}) copy-start(f32[1024,768]{1,0:T(8,128)} %param.24) | copy-start | bytes 9437188
  161.2 6.4 %copy-start.1 = (bf16[4096,384]{1,0:T(8,128)(2,1)S(1)}, bf16[4096,384]{1,0:T(8,128)(2,1)}, u32[]{:S(2)}) copy-start(bf16[4096,384]{1,0:T(8,128)(2,1)} %param.17) | copy-start | bytes 9437188
where the time goes:
time: 168 us
  blocking collectives  100 us (60%)
  matrix products  31.2 us (19%)
  other arithmetic  25.6 us (15%)
  between operations  9.27 us (6%)
    psum x1, blocking collectives, block_step(): lax.psum(jnp.sum(u_blk * u_blk), ('row', 'col')) / (m_total * n_total)  66.2 us
    dot_general x3, matrix products, block_step(): lax.dot_general(act_in, cot_out, CONTRACT_TOKENS, preferred_element_type=...  31.2 us
    psum x1, blocking collectives, block_step(): r_mean = lax.psum(jnp.sum(r_new), 'row') / m_total  24.8 us
    sub x3, other arithmetic, block_step(): return (w_blk - step_size * u_hat, r_new, c_new)  9.92 us
    psum x1, blocking collectives, block_step(): row_sum = lax.psum(jnp.sum(q_blk, axis=1), 'col')  9.05 us
    reduce_sum x3, other arithmetic, block_step(): jnp.sum(u_blk * u_blk)  7.48 us
    reduce_sum x2, other arithmetic, block_step(): jnp.sum(w_blk * w_blk)  6.98 us

commit v1 on v0

v1 whole, which is shorter than its diff:
```python
import functools

import jax
import jax.numpy as jnp
from jax import lax
from jax.experimental import pallas as pl
from jax.experimental.pallas import tpu as pltpu
from jax.sharding import PartitionSpec as P

F32 = jnp.float32
BF16 = jnp.bfloat16
MESH = pl.DeviceIdType.MESH
EPS_SQ = 1e-30
EPS_SCALE = 1e-3
LANES = 128
CONTRACT_TOKENS = (((0,), (0,)), ((), ()))
VMEM_SPEC = pl.BlockSpec(memory_space=pltpu.VMEM)
HBM_SPEC = pl.BlockSpec(memory_space=pltpu.HBM)
SMEM_SPEC = pl.BlockSpec(memory_space=pltpu.SMEM)

DOWN_STEPS = (1, 1, 2, 4)
GATE_STEPS = (4, 4)
UP_STEPS = (4, 4)


def token_dot(act, cot):
    return lax.dot_general(act, cot, CONTRACT_TOKENS, preferred_element_type=F32)


def lane_groups(value):
    parts = [value[:, k : k + LANES] for k in range(0, value.shape[1], LANES)]
    while len(parts) > 1:
        parts = [sum(parts[k : k + 2]) for k in range(0, len(parts), 2)]
    return parts[0]


def update_kernel(row_count, col_count, x_hbm, h_hbm, dg_hbm, du_hbm, do_hbm, wg_hbm, wu_hbm, wd_hbm, rg, cg, ru, cu, rd, cd, beta_ref, step_ref, clip_ref,
                  g_gate, g_up, g_down, w_gate, w_up, w_down, a_gate, a_up, a_down, b_gate, b_up, b_down, rn_gate, cn_gate, rn_up, cn_up, rn_down, cn_down,
                  x_buf, gate_buf, mix_buf, row_gate, row_up, row_down, col_gate, col_up, col_down, tail_buf,
                  load_sem, w_sem, row_send, row_recv, col_send, col_recv, tail_send, tail_recv):
    row_me = lax.axis_index("row")
    col_me = lax.axis_index("col")
    plane = row_count * col_count
    tokens = x_hbm.shape[0]
    unit = tokens // 8
    h_cols = h_hbm.shape[1]
    do_cols = do_hbm.shape[1]

    def row_peer(k):
        return lax.rem(row_me + k, row_count)

    def col_peer(k):
        return lax.rem(col_me + k, col_count)

    barrier = pltpu.get_barrier_semaphore()
    for dc in range(col_count):
        for dr in range(row_count):
            if dc or dr:
                pl.semaphore_signal(barrier, inc=1, device_id={"col": col_peer(dc), "row": row_peer(dr)}, device_id_type=MESH)

    loads = []
    step_no = 0

    def add_steps(steps, make):
        nonlocal step_no
        out = []
        at = 0
        for size in steps:
            lo, n = at * unit, size * unit
            copies = [pltpu.make_async_copy(src.at[pl.ds(lo, n), :], dst, load_sem.at[step_no, k]) for k, (src, dst) in enumerate(make(lo, n))]
            out.append((lo, n, copies))
            loads.append(copies)
            step_no += 1
            at += size
        return out

    down = add_steps(DOWN_STEPS, lambda lo, n: [(h_hbm, mix_buf.at[pl.ds(lo, n), pl.ds(0, h_cols)]), (do_hbm, mix_buf.at[pl.ds(lo, n), pl.ds(h_cols, do_cols)])])
    gate = add_steps(GATE_STEPS, lambda lo, n: [(x_hbm, x_buf.at[pl.ds(lo, n), :]), (dg_hbm, gate_buf.at[pl.ds(lo, n), :])])
    up = add_steps(UP_STEPS, lambda lo, n: [(du_hbm, mix_buf.at[pl.ds(lo, n), :])])
    w_copies = [pltpu.make_async_copy(src, dst, w_sem.at[k]) for k, (src, dst) in enumerate(((wd_hbm, w_down), (wg_hbm, w_gate), (wu_hbm, w_up)))]

    def start(copies):
        for copy in copies:
            copy.start()

    def wait(copies):
        for copy in copies:
            copy.wait()

    def exchange(kind, buf, own, send_sem, recv_sem, index):
        count, me = (col_count, col_me) if kind == "col" else (row_count, row_me)
        peer = col_peer if kind == "col" else row_peer
        buf[pl.ds(me, 1)] = own[None]
        for k in range(1, count):
            pltpu.make_async_remote_copy(buf.at[me], buf.at[me], send_sem.at[index], recv_sem.at[index], device_id={kind: peer(k)}, device_id_type=MESH).start()

        def finish():
            pltpu.make_async_copy(buf.at[pl.ds(0, count - 1)], buf.at[pl.ds(0, count - 1)], send_sem.at[index]).wait()
            pltpu.make_async_copy(buf.at[pl.ds(0, count - 1)], buf.at[pl.ds(0, count - 1)], recv_sem.at[index]).wait()
        return finish

    def sums_out(g, row_buf, col_buf, index):
        q = g * g
        col_part = jnp.sum(q, axis=0, keepdims=True) + q.shape[0] * EPS_SQ
        row_part = jnp.sum(lane_groups(q).T, axis=0, keepdims=True) + q.shape[1] * EPS_SQ
        first = exchange("row", col_buf, col_part, col_send, col_recv, index)
        second = exchange("col", row_buf, row_part, row_send, row_recv, index)
        return first, second

    beta = beta_ref[0]

    def new_stats(finish, g_ref, row_buf, col_buf, r_old, c_old, r_new, c_new, a_ref, b_ref):
        for part in finish:
            part()
        m_total = g_ref.shape[0] * row_count
        n_total = g_ref.shape[1] * col_count
        row_sum = sum(row_buf[k] for k in range(1, col_count)) + row_buf[0]
        col_sum = sum(col_buf[k] for k in range(1, row_count)) + col_buf[0]
        r_val = beta * r_old[...] + (1.0 - beta) * (row_sum / n_total)
        c_val = beta * c_old[...] + (1.0 - beta) * (col_sum / m_total)
        r_new[...] = r_val
        c_new[...] = c_val
        a_row = 1.0 / jnp.sqrt(r_val)
        b_row = 1.0 / jnp.sqrt(c_val)
        a_col = jnp.broadcast_to(a_row, (LANES, a_row.shape[1])).T
        a_ref[...] = a_col
        b_ref[...] = b_row
        t = g_ref[...] * b_row
        u_rows = lane_groups(t * t) * (a_col * a_col)
        return jnp.sum(u_rows, axis=0, keepdims=True), lane_groups(r_val)

    def square_sum(w_ref):
        w = w_ref[...]
        return jnp.sum(lane_groups(w * w), axis=0, keepdims=True)

    for copies in loads[: len(down) + 1]:
        start(copies)

    def matmul(steps, g_ref, act, cot, after):
        for k, (lo, n, copies) in enumerate(steps):
            wait(copies)
            part = token_dot(act(lo, n), cot(lo, n))
            total = part if k == 0 else g_ref[...] + part
            g_ref[...] = total
            after(k)
        return total

    def after_down(k):
        if k == len(down) - 1:
            for item in gate[1:] + up:
                start(item[2])
            start(w_copies)

    total = matmul(down, g_down, lambda lo, n: mix_buf[pl.ds(lo, n), 0:h_cols], lambda lo, n: mix_buf[pl.ds(lo, n), h_cols : h_cols + do_cols], after_down)
    pl.semaphore_wait(barrier, plane - 1)
    down_out = sums_out(total, row_down, col_down, 0)
    total = matmul(gate, g_gate, lambda lo, n: x_buf[pl.ds(lo, n), :], lambda lo, n: gate_buf[pl.ds(lo, n), :], lambda k: None)
    gate_out = sums_out(total, row_gate, col_gate, 1)
    total = matmul(up, g_up, lambda lo, n: x_buf[pl.ds(lo, n), :], lambda lo, n: mix_buf[pl.ds(lo, n), :], lambda k: None)
    up_out = sums_out(total, row_up, col_up, 2)

    wait(w_copies)
    w_sums = [square_sum(w) for w in (w_down, w_gate, w_up)]
    u_down, r_down = new_stats(down_out, g_down, row_down, col_down, rd, cd, rn_down, cn_down, a_down, b_down)
    u_gate, r_gate = new_stats(gate_out, g_gate, row_gate, col_gate, rg, cg, rn_gate, cn_gate, a_gate, b_gate)
    u_up, r_up = new_stats(up_out, g_up, row_up, col_up, ru, cu, rn_up, cn_up, a_up, b_up)

    lane = lax.broadcasted_iota(jnp.int32, (1, LANES), 1)
    packed = jnp.zeros((1, LANES), F32)
    for k, value in enumerate(w_sums + [r_down, r_gate, r_up, u_down, u_gate, u_up]):
        packed = jnp.where(lane == k, jnp.sum(value, axis=1, keepdims=True), packed)
    me = col_me * row_count + row_me
    tail_buf[pl.ds(me, 1)] = packed[None]
    for dc in range(col_count):
        for dr in range(row_count):
            if dc or dr:
                pltpu.make_async_remote_copy(tail_buf.at[me], tail_buf.at[me], tail_send, tail_recv, device_id={"col": col_peer(dc), "row": row_peer(dr)}, device_id_type=MESH).start()
    pltpu.make_async_copy(tail_buf.at[pl.ds(0, plane - 1)], tail_buf.at[pl.ds(0, plane - 1)], tail_send).wait()
    pltpu.make_async_copy(tail_buf.at[pl.ds(0, plane - 1)], tail_buf.at[pl.ds(0, plane - 1)], tail_recv).wait()
    sums = jnp.sum(tail_buf[...], axis=0)

    def pick(k):
        return jnp.sum(jnp.where(lane == k, sums, 0.0), axis=1, keepdims=True)

    for k, (g_ref, a_ref) in enumerate(((g_down, a_down), (g_gate, a_gate), (g_up, a_up))):
        m_total = g_ref.shape[0] * row_count
        n_total = g_ref.shape[1] * col_count
        r_mean = pick(3 + k) / (m_total * col_count)
        w_rms = jnp.sqrt(pick(k) / (m_total * n_total))
        u_rms = jnp.sqrt(r_mean * pick(6 + k) / (m_total * n_total))
        size = step_ref[0] * jnp.maximum(EPS_SCALE, w_rms)
        scale = size * jnp.sqrt(r_mean) / jnp.maximum(1.0, u_rms / clip_ref[0])
        a_ref[...] = a_ref[...] * scale


def apply_kernel(g_gate, g_up, g_down, w_gate, w_up, w_down, a_gate, a_up, a_down, b_gate, b_up, b_down, rn_gate, cn_gate, rn_up, cn_up, rn_down, cn_down,
                 o_gate, o_up, o_down, ro_gate, co_gate, ro_up, co_up, ro_down, co_down, t_gate, t_up, t_down, w_sem, s_sem):
    small = [pltpu.make_async_copy(src, dst, s_sem.at[k]) for k, (src, dst) in enumerate(((rn_gate, ro_gate), (cn_gate, co_gate), (rn_up, ro_up), (cn_up, co_up), (rn_down, ro_down), (cn_down, co_down)))]
    for copy in small:
        copy.start()
    copies = []
    for k, (g, w, a, b, t, o) in enumerate(((g_down, w_down, a_down, b_down, t_down, o_down), (g_gate, w_gate, a_gate, b_gate, t_gate, o_gate), (g_up, w_up, a_up, b_up, t_up, o_up))):
        rows, columns = g.shape
        size = rows // 4
        for part in range(4):
            s = pl.ds(part * size, size)
            a_val = a[s, :]
            for c in range(0, columns, LANES):
                ls = pl.ds(c, LANES)
                t[s, ls] = w[s, ls] - g[s, ls] * (a_val * b[:, ls])
            copy = pltpu.make_async_copy(t.at[s, :], o.at[s, :], w_sem.at[k, part])
            copy.start()
            copies.append(copy)
    for copy in copies + small:
        copy.wait()


def solution(mesh):
    row_count = mesh.shape["row"]
    col_count = mesh.shape["col"]

    def local_program(x_in, h_act, d_gate, d_up, d_out, w_gate, w_up, w_down, r_gate, c_gate, r_up, c_up, r_down, c_down, beta_two, rel_step, clip_thr):
        vec = lambda v: v.reshape(1, -1)
        blocks = (w_gate, w_up, w_down)
        tokens = x_in.shape[0]
        steps = len(DOWN_STEPS) + len(GATE_STEPS) + len(UP_STEPS)
        out_shape = [pltpu.VMEM(w.shape, F32) for w in blocks] * 2
        out_shape += [pltpu.VMEM((w.shape[0], LANES), F32) for w in blocks]
        out_shape += [pltpu.VMEM((1, w.shape[1]), F32) for w in blocks]
        stats = [pltpu.VMEM((1, w.shape[k]), F32) for w in blocks for k in range(2)]
        dma = pltpu.SemaphoreType.DMA
        flops = sum(2 * tokens * w.shape[0] * w.shape[1] for w in blocks)
        mid = pl.pallas_call(
            functools.partial(update_kernel, row_count, col_count),
            out_shape=out_shape + stats,
            in_specs=[HBM_SPEC] * 8 + [VMEM_SPEC] * 6 + [SMEM_SPEC] * 3,
            out_specs=[VMEM_SPEC] * 18,
            scratch_shapes=[
                pltpu.VMEM(x_in.shape, BF16),
                pltpu.VMEM(d_gate.shape, BF16),
                pltpu.VMEM((tokens, max(d_up.shape[1], h_act.shape[1] + d_out.shape[1])), BF16),
                *[pltpu.VMEM((col_count, 1, w.shape[0]), F32) for w in blocks],
                *[pltpu.VMEM((row_count, 1, w.shape[1]), F32) for w in blocks],
                pltpu.VMEM((row_count * col_count, 1, LANES), F32),
                dma((steps, 2)), dma((3,)), dma((3,)), dma((3,)), dma((3,)), dma((3,)), dma, dma,
            ],
            compiler_params=pltpu.CompilerParams(collective_id=0, has_side_effects=True, vmem_limit_bytes=VMEM_A),
            cost_estimate=pl.CostEstimate(flops=flops, bytes_accessed=60_000_000, transcendentals=0),
            name="grad_and_stats",
        )(x_in, h_act, d_gate, d_up, d_out, w_gate, w_up, w_down, vec(r_gate), vec(c_gate), vec(r_up), vec(c_up), vec(r_down), vec(c_down), vec(beta_two)[0], vec(rel_step)[0], vec(clip_thr)[0])
        out = pl.pallas_call(
            apply_kernel,
            out_shape=[jax.ShapeDtypeStruct(w.shape, F32) for w in blocks] + [jax.ShapeDtypeStruct((1, w.shape[k]), F32) for w in blocks for k in range(2)],
            in_specs=[VMEM_SPEC] * 18,
            out_specs=[HBM_SPEC] * 9,
            scratch_shapes=[pltpu.VMEM(w.shape, F32) for w in blocks] + [dma((3, 4)), dma((6,))],
            compiler_params=pltpu.CompilerParams(vmem_limit_bytes=VMEM_B),
            cost_estimate=pl.CostEstimate(flops=10_000_000, bytes_accessed=10_000_000, transcendentals=0),
            name="apply_update",
        )(*mid)
        return tuple(out[:3]) + tuple(v.reshape(-1) for v in out[3:])

    act_spec = P(None, "row")
    cot_spec = P(None, "col")
    w_spec = P("row", "col")
    r_spec = P("row")
    c_spec = P("col")
    s_spec = P()
    return jax.shard_map(local_program, mesh=mesh, in_specs=(act_spec, act_spec, cot_spec, cot_spec, cot_spec, w_spec, w_spec, w_spec, r_spec, c_spec, r_spec, c_spec, r_spec, c_spec, s_spec, s_spec, s_spec), out_specs=(w_spec, w_spec, w_spec, r_spec, c_spec, r_spec, c_spec, r_spec, c_spec), check_vma=False)


VMEM_A = 44 * 2**20
VMEM_B = 14 * 2**20
```

time: 168 us -> 61.1 us (0.36)
  the two profiles are of different devices: /device:TPU:72 before, /device:TPU:1 now
where the time goes in v1:
time: 61.1 us; the launch traced here: 60.8 us
  Pallas kernels  52.7 us (86%)
  local copies, waits for them, and re-layouts  3.76 us (6%)
  between operations  2.6 us (4%)
  other arithmetic  1.8 us (3%)
    pallas_call x1, Pallas kernels, local_program(): pl.pallas_call(functools.partial(update_kernel, row_count, col_count), ou...  48.8 us
    pallas_call x1, Pallas kernels, local_program(): pl.pallas_call(apply_kernel, out_shape=[jax.ShapeDtypeStruct(w.shape, F32...  3.9 us
    reshape x3, local copies, waits for them, and re-layouts, local_program(): vec = lambda v: v.reshape(1, -1)  3.76 us
    pallas_call x3, other arithmetic, local_program(): pl.pallas_call(apply_kernel, out_shape=[jax.ShapeDtypeStruct(w.shape, F32...  1.8 us

profile of v1, /device:TPU:1, one launch (start us, length us, event | category | flops | bytes accessed | tf_op | source)
XLA Modules:
  0.0 60.8 jit_solution(8727247906973362861)
XLA Ops:
  2.6 1.2 %reshape.54.rg = f32[1,384]{1,0:T(1,128)} reshape(f32[384]{0:T(512)} %param.25) | data formatting | bytes 3072 | tf_op jit(solution)/shard_map/reshape | solution.py:223
  3.8 1.2 %reshape.56.ru = f32[1,384]{1,0:T(1,128)} reshape(f32[384]{0:T(512)} %param.27) | data formatting | bytes 3072 | tf_op jit(solution)/shard_map/reshape | solution.py:223
  5.1 1.3 %reshape.59.cd = f32[1,768]{1,0:T(1,128)} reshape(f32[768]{0:T(1024)} %param.30) | data formatting | bytes 6144 | tf_op jit(solution)/shard_map/reshape | solution.py:223
  6.3 48.8 %grad_and_stats.1 = (f32[384,2048]{1,0:T(8,128)S(1)}, f32[384,2048]{1,0:T(8,128)S(1)}, f32[1024,768]{1,0:T(8,128)S(1)}, f32[384,2048]{1,0:T(8,128)S(1)}, f32[384...) custom-call(bf16[4096,384]{1,0:T(8,128)(2,1)} %x_hbm.1, ...), custom_call_target="tpu_custom_call" | custom-call | flops 19327352832 | bytes 60000000 | tf_op jit(solution)/shard_map/grad_and_stats/pallas_call | solution.py:233
  55.1 3.9 %apply_update.1 = (f32[384,2048]{1,0:T(8,128)}, f32[384,2048]{1,0:T(8,128)}, f32[1024,768]{1,0:T(8,128)}, f32[1,384]{1,0:T(1,128)S(1)}, f32[1,2048]{1,0:T(1,128)...) custom-call(f32[384,2048]{1,0:T(8,128)S(1)} %get-tuple-element.36.g_gate, ...), custom_call_target="tpu_custom_call" | custom-call | flops 10000000 | bytes 10000000 | tf_op jit(solution)/shard_map/apply_update/pallas_call | solution.py:251
  59.0 0.6 reduce
  59.6 0.6 reduce.1
  60.2 0.6 reduce.2

commit v2 on v1

v2 whole, which is shorter than its diff:
```python
import functools

import jax
import jax.numpy as jnp
from jax import lax
from jax.experimental import pallas as pl
from jax.experimental.pallas import tpu as pltpu
from jax.sharding import PartitionSpec as P

F32 = jnp.float32
BF16 = jnp.bfloat16
MESH = pl.DeviceIdType.MESH
EPS_SQ = 1e-30
EPS_SCALE = 1e-3
LANES = 128
SUBLANES = 8
CHUNKS = 4
CONTRACT_TOKENS = (((0,), (0,)), ((), ()))
VMEM_SPEC = pl.BlockSpec(memory_space=pltpu.VMEM)
HBM_SPEC = pl.BlockSpec(memory_space=pltpu.HBM)
SMEM_SPEC = pl.BlockSpec(memory_space=pltpu.SMEM)
VMEM_A = 44 * 2**20
VMEM_B = 14 * 2**20


def token_dot(act, cot):
    return lax.dot_general(act, cot, CONTRACT_TOKENS, preferred_element_type=F32)


def tree_sum(parts):
    while len(parts) > 1:
        parts = [sum(parts[k + 1 : k + 2], parts[k]) for k in range(0, len(parts), 2)]
    return parts[0]


def lane_groups(value):
    return tree_sum([value[:, k : k + LANES] for k in range(0, value.shape[1], LANES)])


def row_groups(value):
    return tree_sum([value[k : k + SUBLANES] for k in range(0, value.shape[0], SUBLANES)])


def tile_rows(ref):
    return 32 if ref.shape[1] > 1024 else 64


def over_rows(ref, body, init):
    size = tile_rows(ref)
    return lax.fori_loop(0, ref.shape[0] // size, lambda i, carry: body(pl.ds(pl.multiple_of(i * size, size), size), carry), init)


def update_kernel(row_count, col_count, x_hbm, h_hbm, dg_hbm, du_hbm, do_hbm, wg_hbm, wu_hbm, wd_hbm, rg, cg, ru, cu, rd, cd, beta_ref, step_ref, clip_ref,
                  g_gate, g_up, g_down, w_gate, w_up, w_down, a_gate, a_up, a_down, b_gate, b_up, b_down, rn_gate, cn_gate, rn_up, cn_up, rn_down, cn_down,
                  x_buf, gate_buf, mix_buf, row_gate, row_up, row_down, col_gate, col_up, col_down, tail_buf,
                  old_gate_r, old_gate_c, old_up_r, old_up_c, old_down_r, old_down_c, load_sem, w_sem, small_sem, row_send, row_recv, col_send, col_recv, tail_send, tail_recv):
    row_me = lax.axis_index("row")
    col_me = lax.axis_index("col")
    plane = row_count * col_count
    part = x_hbm.shape[0] // CHUNKS
    h_cols = h_hbm.shape[1]
    do_cols = do_hbm.shape[1]

    def row_peer(k):
        return lax.rem(row_me + k, row_count)

    def col_peer(k):
        return lax.rem(col_me + k, col_count)

    def plane_peers():
        return [{"col": col_peer(dc), "row": row_peer(dr)} for dc in range(col_count) for dr in range(row_count) if dc or dr]

    def start(copies):
        for copy in copies:
            copy.start()

    def wait(copies):
        for copy in copies:
            copy.wait()

    def rows(i):
        return pl.ds(pl.multiple_of(i * part, part), part)

    def load(src, dst, kind, i):
        return pltpu.make_async_copy(src.at[rows(i), :], dst, load_sem.at[kind, i])

    def down_loads(i):
        return [load(h_hbm, mix_buf.at[rows(i), pl.ds(0, h_cols)], 0, i), load(do_hbm, mix_buf.at[rows(i), pl.ds(h_cols, do_cols)], 1, i)]

    def gate_loads(i):
        return [load(x_hbm, x_buf.at[rows(i), :], 2, i), load(dg_hbm, gate_buf.at[rows(i), :], 3, i)]

    def up_loads(i):
        return [load(du_hbm, mix_buf.at[rows(i), :], 4, i)]

    w_copies = [pltpu.make_async_copy(src, dst, w_sem.at[k]) for k, (src, dst) in enumerate(((wd_hbm, w_down), (wg_hbm, w_gate), (wu_hbm, w_up)))]
    stat_copies = [pltpu.make_async_copy(src, dst, small_sem.at[k]) for k, (src, dst) in enumerate(((rg, old_gate_r), (cg, old_gate_c), (ru, old_up_r), (cu, old_up_c), (rd, old_down_r), (cd, old_down_c)))]

    def exchange(kind, buf, own, send_sem, recv_sem, index):
        count, me, peer = (col_count, col_me, col_peer) if kind == "col" else (row_count, row_me, row_peer)
        buf[pl.ds(me, 1)] = own[None]
        for k in range(1, count):
            pltpu.make_async_remote_copy(buf.at[me], buf.at[me], send_sem.at[index], recv_sem.at[index], device_id={kind: peer(k)}, device_id_type=MESH).start()

        def finish():
            for sem in (send_sem, recv_sem):
                pltpu.make_async_copy(buf.at[pl.ds(0, count - 1)], buf.at[pl.ds(0, count - 1)], sem.at[index]).wait()
        return finish

    def sums_out(g_ref, lane_ref, row_buf, col_buf, index):
        def body(s, columns):
            g = g_ref[s, :]
            q = g * g
            lane_ref[s, :] = lane_groups(q)
            return columns + row_groups(q)

        columns = over_rows(g_ref, body, jnp.zeros((SUBLANES, g_ref.shape[1]), F32))
        col_part = jnp.sum(columns, axis=0, keepdims=True) + g_ref.shape[0] * EPS_SQ
        first = exchange("row", col_buf, col_part, col_send, col_recv, index)
        row_part = jnp.sum(lane_ref[...].T, axis=0, keepdims=True) + g_ref.shape[1] * EPS_SQ
        second = exchange("col", row_buf, row_part, row_send, row_recv, index)
        return first, second

    def new_stats(finish, g_ref, row_buf, col_buf, r_old, c_old, r_new, c_new, a_ref, b_ref):
        for part in finish:
            part()
        m_total = g_ref.shape[0] * row_count
        n_total = g_ref.shape[1] * col_count
        beta = beta_ref[...]
        row_sum = tree_sum([row_buf[k] for k in range(col_count)])
        col_sum = tree_sum([col_buf[k] for k in range(row_count)])
        r_val = beta * r_old[...].reshape(1, -1) + (1.0 - beta) * (row_sum / n_total)
        c_val = beta * c_old[...].reshape(1, -1) + (1.0 - beta) * (col_sum / m_total)
        r_new[...] = r_val.reshape(-1)
        c_new[...] = c_val.reshape(-1)
        a_row = 1.0 / jnp.sqrt(r_val)
        b_ref[...] = 1.0 / jnp.sqrt(c_val)
        a_ref[...] = jnp.broadcast_to(a_row, (LANES, a_row.shape[1])).T

        def body(s, total):
            t = g_ref[s, :] * b_ref[...]
            u = lane_groups(t * t) * (a_ref[s, :] * a_ref[s, :])
            return total + row_groups(u)

        return over_rows(g_ref, body, jnp.zeros((SUBLANES, LANES), F32)), lane_groups(r_val)

    def square_sum(w_ref):
        def body(s, total):
            w = w_ref[s, :]
            return total + row_groups(lane_groups(w * w))

        return over_rows(w_ref, body, jnp.zeros((SUBLANES, LANES), F32))

    def matmul(g_ref, loads, act, cot):
        def step(i, carry):
            wait(loads(i))
            product = token_dot(act(rows(i)), cot(rows(i)))
            g_ref[...] = jnp.where(i == 0, 0.0, g_ref[...]) + product
            return carry

        lax.fori_loop(0, CHUNKS, step, 0)

    for i in range(CHUNKS):
        start(down_loads(i))
    for i in range(CHUNKS):
        start(gate_loads(i))
    barrier = pltpu.get_barrier_semaphore()
    for peer in plane_peers():
        pl.semaphore_signal(barrier, inc=1, device_id=peer, device_id_type=MESH)
    matmul(g_down, down_loads, lambda s: mix_buf[s, 0:h_cols], lambda s: mix_buf[s, h_cols : h_cols + do_cols])
    for i in range(CHUNKS):
        start(up_loads(i))
    start(w_copies)
    start(stat_copies)
    pl.semaphore_wait(barrier, plane - 1)
    down_out = sums_out(g_down, a_down, row_down, col_down, 0)
    matmul(g_gate, gate_loads, lambda s: x_buf[s, :], lambda s: gate_buf[s, :])
    gate_out = sums_out(g_gate, a_gate, row_gate, col_gate, 1)
    matmul(g_up, up_loads, lambda s: x_buf[s, :], lambda s: mix_buf[s, :])
    up_out = sums_out(g_up, a_up, row_up, col_up, 2)

    wait(w_copies)
    wait(stat_copies)
    w_sums = [square_sum(w) for w in (w_down, w_gate, w_up)]
    u_down, r_down = new_stats(down_out, g_down, row_down, col_down, old_down_r, old_down_c, rn_down, cn_down, a_down, b_down)
    u_gate, r_gate = new_stats(gate_out, g_gate, row_gate, col_gate, old_gate_r, old_gate_c, rn_gate, cn_gate, a_gate, b_gate)
    u_up, r_up = new_stats(up_out, g_up, row_up, col_up, old_up_r, old_up_c, rn_up, cn_up, a_up, b_up)

    lane = lax.broadcasted_iota(jnp.int32, (1, LANES), 1)
    packed = jnp.zeros((1, LANES), F32)
    for k, value in enumerate(w_sums + [r_down, r_gate, r_up, u_down, u_gate, u_up]):
        packed = jnp.where(lane == k, jnp.sum(jnp.sum(value, axis=0, keepdims=True), axis=1, keepdims=True), packed)
    me = col_me * row_count + row_me
    tail_buf[pl.ds(me, 1)] = packed[None]
    for peer in plane_peers():
        pltpu.make_async_remote_copy(tail_buf.at[me], tail_buf.at[me], tail_send, tail_recv, device_id=peer, device_id_type=MESH).start()
    for sem in (tail_send, tail_recv):
        pltpu.make_async_copy(tail_buf.at[pl.ds(0, plane - 1)], tail_buf.at[pl.ds(0, plane - 1)], sem).wait()
    sums = jnp.sum(tail_buf[...], axis=0)

    def pick(k):
        return jnp.sum(jnp.where(lane == k, sums, 0.0), axis=1, keepdims=True)

    for k, (g_ref, a_ref) in enumerate(((g_down, a_down), (g_gate, a_gate), (g_up, a_up))):
        m_total = g_ref.shape[0] * row_count
        n_total = g_ref.shape[1] * col_count
        r_mean = pick(3 + k) / (m_total * col_count)
        w_rms = jnp.sqrt(pick(k) / (m_total * n_total))
        u_rms = jnp.sqrt(r_mean * pick(6 + k) / (m_total * n_total))
        size = step_ref[...] * jnp.maximum(EPS_SCALE, w_rms)
        scale = size * jnp.sqrt(r_mean) / jnp.maximum(1.0, u_rms / clip_ref[...])
        a_ref[...] = a_ref[...] * scale


PARTS = 4


def apply_kernel(g_gate, g_up, g_down, w_gate, w_up, w_down, a_gate, a_up, a_down, b_gate, b_up, b_down, rn_gate, cn_gate, rn_up, cn_up, rn_down, cn_down,
                 o_gate, o_up, o_down, ro_gate, co_gate, ro_up, co_up, ro_down, co_down, t_gate, t_up, t_down, w_sem, s_sem):
    small = [pltpu.make_async_copy(src, dst, s_sem.at[k]) for k, (src, dst) in enumerate(((rn_gate, ro_gate), (cn_gate, co_gate), (rn_up, ro_up), (cn_up, co_up), (rn_down, ro_down), (cn_down, co_down)))]
    for copy in small:
        copy.start()
    blocks = ((g_down, w_down, a_down, b_down, t_down, o_down), (g_gate, w_gate, a_gate, b_gate, t_gate, o_gate), (g_up, w_up, a_up, b_up, t_up, o_up))

    def out_copy(k, i):
        t, o = blocks[k][4:]
        size = t.shape[0] // PARTS
        s = pl.ds(pl.multiple_of(i * size, size), size)
        return pltpu.make_async_copy(t.at[s, :], o.at[s, :], w_sem.at[k, i])

    for k, (g, w, a, b, t, o) in enumerate(blocks):
        size = g.shape[0] // PARTS
        tile = tile_rows(g)

        def part(i, carry):
            def body(j, inner):
                s = pl.ds(pl.multiple_of(i * size + j * tile, tile), tile)
                a_val = a[s, :]
                for c in range(0, g.shape[1], LANES):
                    ls = pl.ds(c, LANES)
                    t[s, ls] = w[s, ls] - g[s, ls] * (a_val * b[:, ls])
                return inner

            lax.fori_loop(0, size // tile, body, 0)
            out_copy(k, i).start()
            return carry

        lax.fori_loop(0, PARTS, part, 0)
    for k in range(len(blocks)):
        for i in range(PARTS):
            out_copy(k, i).wait()
    for copy in small:
        copy.wait()


def solution(mesh):
    row_count = mesh.shape["row"]
    col_count = mesh.shape["col"]

    def local_program(x_in, h_act, d_gate, d_up, d_out, w_gate, w_up, w_down, r_gate, c_gate, r_up, c_up, r_down, c_down, beta_two, rel_step, clip_thr):
        blocks = (w_gate, w_up, w_down)
        tokens = x_in.shape[0]
        out_shape = [pltpu.VMEM(w.shape, F32) for w in blocks] * 2
        out_shape += [pltpu.VMEM((w.shape[0], LANES), F32) for w in blocks]
        out_shape += [pltpu.VMEM((1, w.shape[1]), F32) for w in blocks]
        stats = [pltpu.VMEM((w.shape[k],), F32) for w in blocks for k in range(2)]
        dma = pltpu.SemaphoreType.DMA
        flops = sum(2 * tokens * w.shape[0] * w.shape[1] for w in blocks)
        mid = pl.pallas_call(
            functools.partial(update_kernel, row_count, col_count),
            out_shape=out_shape + stats,
            in_specs=[HBM_SPEC] * 14 + [SMEM_SPEC] * 3,
            out_specs=[VMEM_SPEC] * 18,
            scratch_shapes=[
                pltpu.VMEM(x_in.shape, BF16),
                pltpu.VMEM(d_gate.shape, BF16),
                pltpu.VMEM((tokens, max(d_up.shape[1], h_act.shape[1] + d_out.shape[1])), BF16),
                *[pltpu.VMEM((col_count, 1, w.shape[0]), F32) for w in blocks],
                *[pltpu.VMEM((row_count, 1, w.shape[1]), F32) for w in blocks],
                pltpu.VMEM((row_count * col_count, 1, LANES), F32),
                *[pltpu.VMEM((w.shape[k],), F32) for w in blocks for k in range(2)],
                dma((5, CHUNKS)), dma((3,)), dma((6,)), dma((3,)), dma((3,)), dma((3,)), dma((3,)), dma, dma,
            ],
            compiler_params=pltpu.CompilerParams(collective_id=0, has_side_effects=True, vmem_limit_bytes=VMEM_A),
            cost_estimate=pl.CostEstimate(flops=flops, bytes_accessed=60_000_000, transcendentals=0),
            name="grad_and_stats",
        )(x_in, h_act, d_gate, d_up, d_out, w_gate, w_up, w_down, r_gate, c_gate, r_up, c_up, r_down, c_down, beta_two, rel_step, clip_thr)
        out = pl.pallas_call(
            apply_kernel,
            out_shape=[jax.ShapeDtypeStruct(w.shape, F32) for w in blocks] + [jax.ShapeDtypeStruct((w.shape[k],), F32) for w in blocks for k in range(2)],
            in_specs=[VMEM_SPEC] * 18,
            out_specs=[HBM_SPEC] * 9,
            scratch_shapes=[pltpu.VMEM(w.shape, F32) for w in blocks] + [dma((3, PARTS)), dma((6,))],
            compiler_params=pltpu.CompilerParams(vmem_limit_bytes=VMEM_B),
            cost_estimate=pl.CostEstimate(flops=10_000_000, bytes_accessed=10_000_000, transcendentals=0),
            name="apply_update",
        )(*mid)
        return tuple(out)

    act_spec = P(None, "row")
    cot_spec = P(None, "col")
    w_spec = P("row", "col")
    r_spec = P("row")
    c_spec = P("col")
    s_spec = P()
    return jax.shard_map(local_program, mesh=mesh, in_specs=(act_spec, act_spec, cot_spec, cot_spec, cot_spec, w_spec, w_spec, w_spec, r_spec, c_spec, r_spec, c_spec, r_spec, c_spec, s_spec, s_spec, s_spec), out_specs=(w_spec, w_spec, w_spec, r_spec, c_spec, r_spec, c_spec, r_spec, c_spec), check_vma=False)
```

time: 61.1 us -> 45.2 us (0.74)
  Pallas kernels: 52.7 us -> 42.5 us
  local copies, waits for them, and re-layouts: 3.76 us -> 0 us
  other arithmetic: 1.8 us -> 0 us
    pallas_call x1, Pallas kernels: 48.8 us -> 38.5 us  [local_program(): pl.pallas_call(functools.partial(update_kernel, row_count, col_count), ou...]
    reshape x3 -> x0, local copies, waits for them, and re-layouts: 3.76 us -> none  [local_program(): vec = lambda v: v.reshape(1, -1)]
    pallas_call x3 -> x0, other arithmetic: 1.8 us -> none  [local_program(): pl.pallas_call(apply_kernel, out_shape=[jax.ShapeDtypeStruct(w.shape, F32...]
where the time goes in v2:
time: 45.2 us; the launch traced here: 45 us
  Pallas kernels  42.5 us (94%)
  between operations  2.59 us (6%)
    pallas_call x1, Pallas kernels, local_program(): pl.pallas_call(functools.partial(update_kernel, row_count, col_count), ou...  38.5 us
    pallas_call x1, Pallas kernels, local_program(): pl.pallas_call(apply_kernel, out_shape=[jax.ShapeDtypeStruct(w.shape, F32...  3.91 us

profile of v2, /device:TPU:1, one launch (start us, length us, event | category | flops | bytes accessed | tf_op | source)
XLA Modules:
  0.0 45.0 jit_solution(14559980028095306310)
XLA Ops:
  2.6 38.5 %grad_and_stats.1 = (f32[384,2048]{1,0:T(8,128)S(1)}, f32[384,2048]{1,0:T(8,128)S(1)}, f32[1024,768]{1,0:T(8,128)S(1)}, f32[384,2048]{1,0:T(8,128)S(1)}, f32[384...) custom-call(bf16[4096,384]{1,0:T(8,128)(2,1)} %x_hbm.1, ...), custom_call_target="tpu_custom_call" | custom-call | flops 19327352832 | bytes 60000000 | tf_op jit(solution)/shard_map/grad_and_stats/pallas_call | solution.py:269
  41.1 3.9 %apply_update.1 = (f32[384,2048]{1,0:T(8,128)}, f32[384,2048]{1,0:T(8,128)}, f32[1024,768]{1,0:T(8,128)}, f32[384]{0:T(512)}, f32[2048]{0:T(1024)}, /*index=5*/f...) custom-call(f32[384,2048]{1,0:T(8,128)S(1)} %get-tuple-element.27.g_gate, ...), custom_call_target="tpu_custom_call" | custom-call | flops 10000000 | bytes 10000000 | tf_op jit(solution)/shard_map/apply_update/pallas_call | solution.py:288

commit v3 on v2

--- a/solution.py
+++ b/solution.py
@@ -14,7 +14,9 @@
 EPS_SCALE = 1e-3
 LANES = 128
 SUBLANES = 8
-CHUNKS = 4
+DOWN_CHUNKS = 4
+GATE_CHUNKS = 2
+UP_CHUNKS = 2
 CONTRACT_TOKENS = (((0,), (0,)), ((), ()))
 VMEM_SPEC = pl.BlockSpec(memory_space=pltpu.VMEM)
 HBM_SPEC = pl.BlockSpec(memory_space=pltpu.HBM)
@@ -42,7 +44,7 @@
 
 
 def tile_rows(ref):
-    return 32 if ref.shape[1] > 1024 else 64
+    return 64 if ref.shape[1] > 1024 else 128
 
 
 def over_rows(ref, body, init):
@@ -57,7 +59,7 @@
     row_me = lax.axis_index("row")
     col_me = lax.axis_index("col")
     plane = row_count * col_count
-    part = x_hbm.shape[0] // CHUNKS
+    tokens = x_hbm.shape[0]
     h_cols = h_hbm.shape[1]
     do_cols = do_hbm.shape[1]
 
@@ -78,20 +80,23 @@
         for copy in copies:
             copy.wait()
 
-    def rows(i):
-        return pl.ds(pl.multiple_of(i * part, part), part)
-
-    def load(src, dst, kind, i):
-        return pltpu.make_async_copy(src.at[rows(i), :], dst, load_sem.at[kind, i])
+    def rows(i, count):
+        return pl.ds(pl.multiple_of(i * (tokens // count), tokens // count), tokens // count)
+
+    def load(src, dst, s, kind, i):
+        return pltpu.make_async_copy(src.at[s, :], dst, load_sem.at[kind, i])
 
     def down_loads(i):
-        return [load(h_hbm, mix_buf.at[rows(i), pl.ds(0, h_cols)], 0, i), load(do_hbm, mix_buf.at[rows(i), pl.ds(h_cols, do_cols)], 1, i)]
+        s = rows(i, DOWN_CHUNKS)
+        return [load(h_hbm, mix_buf.at[s, pl.ds(0, h_cols)], s, 0, i), load(do_hbm, mix_buf.at[s, pl.ds(h_cols, do_cols)], s, 1, i)]
 
     def gate_loads(i):
-        return [load(x_hbm, x_buf.at[rows(i), :], 2, i), load(dg_hbm, gate_buf.at[rows(i), :], 3, i)]
+        s = rows(i, GATE_CHUNKS)
+        return [load(x_hbm, x_buf.at[s, :], s, 2, i), load(dg_hbm, gate_buf.at[s, :], s, 3, i)]
 
     def up_loads(i):
-        return [load(du_hbm, mix_buf.at[rows(i), :], 4, i)]
+        s = rows(i, UP_CHUNKS)
+        return [load(du_hbm, mix_buf.at[s, :], s, 4, i)]
 
     w_copies = [pltpu.make_async_copy(src, dst, w_sem.at[k]) for k, (src, dst) in enumerate(((wd_hbm, w_down), (wg_hbm, w_gate), (wu_hbm, w_up)))]
     stat_copies = [pltpu.make_async_copy(src, dst, small_sem.at[k]) for k, (src, dst) in enumerate(((rg, old_gate_r), (cg, old_gate_c), (ru, old_up_r), (cu, old_up_c), (rd, old_down_r), (cd, old_down_c)))]
@@ -107,14 +112,16 @@
                 pltpu.make_async_copy(buf.at[pl.ds(0, count - 1)], buf.at[pl.ds(0, count - 1)], sem.at[index]).wait()
         return finish
 
-    def sums_out(g_ref, lane_ref, row_buf, col_buf, index):
-        def body(s, columns):
-            g = g_ref[s, :]
-            q = g * g
-            lane_ref[s, :] = lane_groups(q)
-            return columns + row_groups(q)
-
-        columns = over_rows(g_ref, body, jnp.zeros((SUBLANES, g_ref.shape[1]), F32))
+    def block_sums(g_ref, lane_ref, s, columns):
+        g = g_ref[s, :]
+        q = g * g
+        lane_ref[s, :] = lane_groups(q)
+        return columns + row_groups(q)
+
+    def no_columns(g_ref):
+        return jnp.zeros((SUBLANES, g_ref.shape[1]), F32)
+
+    def send_sums(columns, g_ref, lane_ref, row_buf, col_buf, index):
         col_part = jnp.sum(columns, axis=0, keepdims=True) + g_ref.shape[0] * EPS_SQ
         first = exchange("row", col_buf, col_part, col_send, col_recv, index)
         row_part = jnp.sum(lane_ref[...].T, axis=0, keepdims=True) + g_ref.shape[1] * EPS_SQ
@@ -151,33 +158,42 @@
 
         return over_rows(w_ref, body, jnp.zeros((SUBLANES, LANES), F32))
 
-    def matmul(g_ref, loads, act, cot):
+    def matmul(g_ref, count, loads, act, cot, beside, init):
         def step(i, carry):
             wait(loads(i))
-            product = token_dot(act(rows(i)), cot(rows(i)))
+            carry = beside(i, carry)
+            product = token_dot(act(rows(i, count)), cot(rows(i, count)))
             g_ref[...] = jnp.where(i == 0, 0.0, g_ref[...]) + product
             return carry
 
-        lax.fori_loop(0, CHUNKS, step, 0)
-
-    for i in range(CHUNKS):
+        return lax.fori_loop(0, count, step, init)
+
+    for i in range(DOWN_CHUNKS):
         start(down_loads(i))
-    for i in range(CHUNKS):
+    for i in range(GATE_CHUNKS):
         start(gate_loads(i))
     barrier = pltpu.get_barrier_semaphore()
     for peer in plane_peers():
         pl.semaphore_signal(barrier, inc=1, device_id=peer, device_id_type=MESH)
-    matmul(g_down, down_loads, lambda s: mix_buf[s, 0:h_cols], lambda s: mix_buf[s, h_cols : h_cols + do_cols])
-    for i in range(CHUNKS):
+    matmul(g_down, DOWN_CHUNKS, down_loads, lambda s: mix_buf[s, 0:h_cols], lambda s: mix_buf[s, h_cols : h_cols + do_cols], lambda i, c: c, 0)
+    for i in range(UP_CHUNKS):
         start(up_loads(i))
     start(w_copies)
     start(stat_copies)
     pl.semaphore_wait(barrier, plane - 1)
-    down_out = sums_out(g_down, a_down, row_down, col_down, 0)
-    matmul(g_gate, gate_loads, lambda s: x_buf[s, :], lambda s: gate_buf[s, :])
-    gate_out = sums_out(g_gate, a_gate, row_gate, col_gate, 1)
-    matmul(g_up, up_loads, lambda s: x_buf[s, :], lambda s: mix_buf[s, :])
-    up_out = sums_out(g_up, a_up, row_up, col_up, 2)
+
+    def down_sums(i, columns):
+        size = g_down.shape[0] // GATE_CHUNKS
+        return block_sums(g_down, a_down, pl.ds(pl.multiple_of(i * size, size), size), columns)
+
+    columns = matmul(g_gate, GATE_CHUNKS, gate_loads, lambda s: x_buf[s, :], lambda s: gate_buf[s, :], down_sums, no_columns(g_down))
+    down_out = send_sums(columns, g_down, a_down, row_down, col_down, 0)
+    columns = over_rows(g_gate, lambda s, c: block_sums(g_gate, a_gate, s, c), no_columns(g_gate))
+    gate_out = send_sums(columns, g_gate, a_gate, row_gate, col_gate, 1)
+
+    matmul(g_up, UP_CHUNKS, up_loads, lambda s: x_buf[s, :], lambda s: mix_buf[s, :], lambda i, c: c, 0)
+    columns = over_rows(g_up, lambda s, c: block_sums(g_up, a_up, s, c), no_columns(g_up))
+    up_out = send_sums(columns, g_up, a_up, row_up, col_up, 2)
 
     wait(w_copies)
     wait(stat_copies)
@@ -230,7 +246,7 @@
 
     for k, (g, w, a, b, t, o) in enumerate(blocks):
         size = g.shape[0] // PARTS
-        tile = tile_rows(g)
+        tile = min(tile_rows(g) // 2, size)
 
         def part(i, carry):
             def body(j, inner):
@@ -279,7 +295,7 @@
                 *[pltpu.VMEM((row_count, 1, w.shape[1]), F32) for w in blocks],
                 pltpu.VMEM((row_count * col_count, 1, LANES), F32),
                 *[pltpu.VMEM((w.shape[k],), F32) for w in blocks for k in range(2)],
-                dma((5, CHUNKS)), dma((3,)), dma((6,)), dma((3,)), dma((3,)), dma((3,)), dma((3,)), dma, dma,
+                dma((5, 4)), dma((3,)), dma((6,)), dma((3,)), dma((3,)), dma((3,)), dma((3,)), dma, dma,
             ],
             compiler_params=pltpu.CompilerParams(collective_id=0, has_side_effects=True, vmem_limit_bytes=VMEM_A),
             cost_estimate=pl.CostEstimate(flops=flops, bytes_accessed=60_000_000, transcendentals=0),

time: 45.2 us -> 44.7 us (0.989)
  Pallas kernels: 42.5 us -> 41.9 us
    pallas_call x1, Pallas kernels: 38.5 us -> 38 us  [local_program(): pl.pallas_call(functools.partial(update_kernel, row_count, col_count), ou...]
where the time goes in v3:
time: 44.7 us; the launch traced here: 44.5 us
  Pallas kernels  41.9 us (94%)
  between operations  2.59 us (6%)
    pallas_call x1, Pallas kernels, local_program(): pl.pallas_call(functools.partial(update_kernel, row_count, col_count), ou...  38 us
    pallas_call x1, Pallas kernels, local_program(): pl.pallas_call(apply_kernel, out_shape=[jax.ShapeDtypeStruct(w.shape, F32...  3.91 us

profile of v3, /device:TPU:1, one launch (start us, length us, event | category | flops | bytes accessed | tf_op | source)
XLA Modules:
  0.0 44.5 jit_solution(17190087871089855886)
XLA Ops:
  2.6 38.0 %grad_and_stats.1 = (f32[384,2048]{1,0:T(8,128)S(1)}, f32[384,2048]{1,0:T(8,128)S(1)}, f32[1024,768]{1,0:T(8,128)S(1)}, f32[384,2048]{1,0:T(8,128)S(1)}, f32[384...) custom-call(bf16[4096,384]{1,0:T(8,128)(2,1)} %x_hbm.1, ...), custom_call_target="tpu_custom_call" | custom-call | flops 19327352832 | bytes 60000000 | tf_op jit(solution)/shard_map/grad_and_stats/pallas_call | solution.py:285
  40.6 3.9 %apply_update.1 = (f32[384,2048]{1,0:T(8,128)}, f32[384,2048]{1,0:T(8,128)}, f32[1024,768]{1,0:T(8,128)}, f32[384]{0:T(512)}, f32[2048]{0:T(1024)}, /*index=5*/f...) custom-call(f32[384,2048]{1,0:T(8,128)S(1)} %get-tuple-element.27.g_gate, ...), custom_call_target="tpu_custom_call" | custom-call | flops 10000000 | bytes 10000000 | tf_op jit(solution)/shard_map/apply_update/pallas_call | solution.py:304

commit v4 on v3

--- a/solution.py
+++ b/solution.py
@@ -69,8 +69,13 @@
     def col_peer(k):
         return lax.rem(col_me + k, col_count)
 
+    def farthest_first(count):
+        return sorted(range(1, count), key=lambda k: -min(k, count - k))
+
     def plane_peers():
-        return [{"col": col_peer(dc), "row": row_peer(dr)} for dc in range(col_count) for dr in range(row_count) if dc or dr]
+        offsets = [(dc, dr) for dc in range(col_count) for dr in range(row_count) if dc or dr]
+        offsets.sort(key=lambda o: -min(o[0], col_count - o[0]) - min(o[1], row_count - o[1]) / 2)
+        return [{"col": col_peer(dc), "row": row_peer(dr)} for dc, dr in offsets]
 
     def start(copies):
         for copy in copies:
@@ -104,7 +109,7 @@
     def exchange(kind, buf, own, send_sem, recv_sem, index):
         count, me, peer = (col_count, col_me, col_peer) if kind == "col" else (row_count, row_me, row_peer)
         buf[pl.ds(me, 1)] = own[None]
-        for k in range(1, count):
+        for k in farthest_first(count):
             pltpu.make_async_remote_copy(buf.at[me], buf.at[me], send_sem.at[index], recv_sem.at[index], device_id={kind: peer(k)}, device_id_type=MESH).start()
 
         def finish():
@@ -123,26 +128,27 @@
 
     def send_sums(columns, g_ref, lane_ref, row_buf, col_buf, index):
         col_part = jnp.sum(columns, axis=0, keepdims=True) + g_ref.shape[0] * EPS_SQ
+        row_part = jnp.sum(lane_ref[...].T, axis=0, keepdims=True) + g_ref.shape[1] * EPS_SQ
         first = exchange("row", col_buf, col_part, col_send, col_recv, index)
-        row_part = jnp.sum(lane_ref[...].T, axis=0, keepdims=True) + g_ref.shape[1] * EPS_SQ
         second = exchange("col", row_buf, row_part, row_send, row_recv, index)
         return first, second
 
     def new_stats(finish, g_ref, row_buf, col_buf, r_old, c_old, r_new, c_new, a_ref, b_ref):
-        for part in finish:
-            part()
+        finish_columns, finish_rows = finish
+        finish_rows()
         m_total = g_ref.shape[0] * row_count
         n_total = g_ref.shape[1] * col_count
         beta = beta_ref[...]
         row_sum = tree_sum([row_buf[k] for k in range(col_count)])
+        r_val = beta * r_old[...].reshape(1, -1) + (1.0 - beta) * (row_sum / n_total)
+        r_new[...] = r_val.reshape(-1)
+        a_row = 1.0 / jnp.sqrt(r_val)
+        a_ref[...] = jnp.broadcast_to(a_row, (LANES, a_row.shape[1])).T
+        finish_columns()
         col_sum = tree_sum([col_buf[k] for k in range(row_count)])
-        r_val = beta * r_old[...].reshape(1, -1) + (1.0 - beta) * (row_sum / n_total)
         c_val = beta * c_old[...].reshape(1, -1) + (1.0 - beta) * (col_sum / m_total)
-        r_new[...] = r_val.reshape(-1)
         c_new[...] = c_val.reshape(-1)
-        a_row = 1.0 / jnp.sqrt(r_val)
         b_ref[...] = 1.0 / jnp.sqrt(c_val)
-        a_ref[...] = jnp.broadcast_to(a_row, (LANES, a_row.shape[1])).T
 
         def body(s, total):
             t = g_ref[s, :] * b_ref[...]

time: 44.7 us -> 44.5 us (level)
  no operation moved by 1% of the time
where the time goes in v4:
time: 44.5 us; the launch traced here: 44.4 us
  Pallas kernels  41.8 us (94%)
  between operations  2.59 us (6%)
    pallas_call x1, Pallas kernels, local_program(): pl.pallas_call(functools.partial(update_kernel, row_count, col_count), ou...  37.9 us
    pallas_call x1, Pallas kernels, local_program(): pl.pallas_call(apply_kernel, out_shape=[jax.ShapeDtypeStruct(w.shape, F32...  3.91 us

profile of v4, /device:TPU:1, one launch (start us, length us, event | category | flops | bytes accessed | tf_op | source)
XLA Modules:
  0.0 44.4 jit_solution(10888279858107895756)
XLA Ops:
  2.6 37.9 %grad_and_stats.1 = (f32[384,2048]{1,0:T(8,128)S(1)}, f32[384,2048]{1,0:T(8,128)S(1)}, f32[1024,768]{1,0:T(8,128)S(1)}, f32[384,2048]{1,0:T(8,128)S(1)}, f32[384...) custom-call(bf16[4096,384]{1,0:T(8,128)(2,1)} %x_hbm.1, ...), custom_call_target="tpu_custom_call" | custom-call | flops 19327352832 | bytes 60000000 | tf_op jit(solution)/shard_map/grad_and_stats/pallas_call | solution.py:291
  40.4 3.9 %apply_update.1 = (f32[384,2048]{1,0:T(8,128)}, f32[384,2048]{1,0:T(8,128)}, f32[1024,768]{1,0:T(8,128)}, f32[384]{0:T(512)}, f32[2048]{0:T(1024)}, /*index=5*/f...) custom-call(f32[384,2048]{1,0:T(8,128)S(1)} %get-tuple-element.27.g_gate, ...), custom_call_target="tpu_custom_call" | custom-call | flops 10000000 | bytes 10000000 | tf_op jit(solution)/shard_map/apply_update/pallas_call | solution.py:310

commit v5 on v4

--- a/solution.py
+++ b/solution.py
@@ -14,7 +14,6 @@
 EPS_SCALE = 1e-3
 LANES = 128
 SUBLANES = 8
-DOWN_CHUNKS = 4
 GATE_CHUNKS = 2
 UP_CHUNKS = 2
 CONTRACT_TOKENS = (((0,), (0,)), ((), ()))
@@ -91,9 +90,21 @@
     def load(src, dst, s, kind, i):
         return pltpu.make_async_copy(src.at[s, :], dst, load_sem.at[kind, i])
 
-    def down_loads(i):
-        s = rows(i, DOWN_CHUNKS)
-        return [load(h_hbm, mix_buf.at[s, pl.ds(0, h_cols)], s, 0, i), load(do_hbm, mix_buf.at[s, pl.ds(h_cols, do_cols)], s, 1, i)]
+    def head_rows(i, count=None):
+        return rows(i, 8)
+
+    def rest_rows(i, count=None):
+        size = 3 * tokens // 8
+        return pl.ds(pl.multiple_of(tokens // 4 + i * size, tokens // 8), size)
+
+    def down_load_pair(s, kind, i):
+        return [load(h_hbm, mix_buf.at[s, pl.ds(0, h_cols)], s, kind, i), load(do_hbm, mix_buf.at[s, pl.ds(h_cols, do_cols)], s, kind + 1, i)]
+
+    def head_loads(i):
+        return down_load_pair(head_rows(i), 0, i)
+
+    def rest_loads(i):
+        return down_load_pair(rest_rows(i), 5, i)
 
     def gate_loads(i):
         s = rows(i, GATE_CHUNKS)
@@ -164,24 +175,30 @@
 
         return over_rows(w_ref, body, jnp.zeros((SUBLANES, LANES), F32))
 
-    def matmul(g_ref, count, loads, act, cot, beside, init):
+    def matmul(g_ref, count, loads, act, cot, beside, init, pick=rows, clear=True):
         def step(i, carry):
             wait(loads(i))
             carry = beside(i, carry)
-            product = token_dot(act(rows(i, count)), cot(rows(i, count)))
-            g_ref[...] = jnp.where(i == 0, 0.0, g_ref[...]) + product
+            s = pick(i, count)
+            product = token_dot(act(s), cot(s))
+            g_ref[...] = (jnp.where(i == 0, 0.0, g_ref[...]) if clear else g_ref[...]) + product
             return carry
 
         return lax.fori_loop(0, count, step, init)
 
-    for i in range(DOWN_CHUNKS):
-        start(down_loads(i))
+    for i in range(2):
+        start(head_loads(i))
+    for i in range(2):
+        start(rest_loads(i))
     for i in range(GATE_CHUNKS):
         start(gate_loads(i))
     barrier = pltpu.get_barrier_semaphore()
     for peer in plane_peers():
         pl.semaphore_signal(barrier, inc=1, device_id=peer, device_id_type=MESH)
-    matmul(g_down, DOWN_CHUNKS, down_loads, lambda s: mix_buf[s, 0:h_cols], lambda s: mix_buf[s, h_cols : h_cols + do_cols], lambda i, c: c, 0)
+    down_act = lambda s: mix_buf[s, 0:h_cols]
+    down_cot = lambda s: mix_buf[s, h_cols : h_cols + do_cols]
+    matmul(g_down, 2, head_loads, down_act, down_cot, lambda i, c: c, 0, head_rows)
+    matmul(g_down, 2, rest_loads, down_act, down_cot, lambda i, c: c, 0, rest_rows, False)
     for i in range(UP_CHUNKS):
         start(up_loads(i))
     start(w_copies)
@@ -301,7 +318,7 @@
                 *[pltpu.VMEM((row_count, 1, w.shape[1]), F32) for w in blocks],
                 pltpu.VMEM((row_count * col_count, 1, LANES), F32),
                 *[pltpu.VMEM((w.shape[k],), F32) for w in blocks for k in range(2)],
-                dma((5, 4)), dma((3,)), dma((6,)), dma((3,)), dma((3,)), dma((3,)), dma((3,)), dma, dma,
+                dma((7, 4)), dma((3,)), dma((6,)), dma((3,)), dma((3,)), dma((3,)), dma((3,)), dma, dma,
             ],
             compiler_params=pltpu.CompilerParams(collective_id=0, has_side_effects=True, vmem_limit_bytes=VMEM_A),
             cost_estimate=pl.CostEstimate(flops=flops, bytes_accessed=60_000_000, transcendentals=0),

time: 44.5 us -> 43.9 us (0.987)
  Pallas kernels: 41.8 us -> 41.2 us
    pallas_call x1, Pallas kernels: 37.9 us -> 37.3 us  [local_program(): pl.pallas_call(functools.partial(update_kernel, row_count, col_count), ou...]
where the time goes in v5:
time: 43.9 us; the launch traced here: 43.8 us
  Pallas kernels  41.2 us (94%)
  between operations  2.59 us (6%)
    pallas_call x1, Pallas kernels, local_program(): pl.pallas_call(functools.partial(update_kernel, row_count, col_count), ou...  37.3 us
    pallas_call x1, Pallas kernels, local_program(): pl.pallas_call(apply_kernel, out_shape=[jax.ShapeDtypeStruct(w.shape, F32...  3.91 us

profile of v5, /device:TPU:1, one launch (start us, length us, event | category | flops | bytes accessed | tf_op | source)
XLA Modules:
  0.0 43.8 jit_solution(9981222518268126156)
XLA Ops:
  2.6 37.3 %grad_and_stats.1 = (f32[384,2048]{1,0:T(8,128)S(1)}, f32[384,2048]{1,0:T(8,128)S(1)}, f32[1024,768]{1,0:T(8,128)S(1)}, f32[384,2048]{1,0:T(8,128)S(1)}, f32[384...) custom-call(bf16[4096,384]{1,0:T(8,128)(2,1)} %x_hbm.1, ...), custom_call_target="tpu_custom_call" | custom-call | flops 19327352832 | bytes 60000000 | tf_op jit(solution)/shard_map/grad_and_stats/pallas_call | solution.py:308
  39.9 3.9 %apply_update.1 = (f32[384,2048]{1,0:T(8,128)}, f32[384,2048]{1,0:T(8,128)}, f32[1024,768]{1,0:T(8,128)}, f32[384]{0:T(512)}, f32[2048]{0:T(1024)}, /*index=5*/f...) custom-call(f32[384,2048]{1,0:T(8,128)S(1)} %get-tuple-element.27.g_gate, ...), custom_call_target="tpu_custom_call" | custom-call | flops 10000000 | bytes 10000000 | tf_op jit(solution)/shard_map/apply_update/pallas_call | solution.py:327

commit v6 on v5

--- a/solution.py
+++ b/solution.py
@@ -43,7 +43,7 @@
 
 
 def tile_rows(ref):
-    return 64 if ref.shape[1] > 1024 else 128
+    return 128 if ref.shape[1] > 1024 else 256
 
 
 def over_rows(ref, body, init):
@@ -269,7 +269,7 @@
 
     for k, (g, w, a, b, t, o) in enumerate(blocks):
         size = g.shape[0] // PARTS
-        tile = min(tile_rows(g) // 2, size)
+        tile = min(tile_rows(g) // 4, size)
 
         def part(i, carry):
             def body(j, inner):

time: 43.9 us -> 43.9 us (level)
  no operation moved by 1% of the time
where the time goes in v6:
time: 43.9 us; the launch traced here: 43.8 us
  Pallas kernels  41.2 us (94%)
  between operations  2.59 us (6%)
    pallas_call x1, Pallas kernels, local_program(): pl.pallas_call(functools.partial(update_kernel, row_count, col_count), ou...  37.3 us
    pallas_call x1, Pallas kernels, local_program(): pl.pallas_call(apply_kernel, out_shape=[jax.ShapeDtypeStruct(w.shape, F32...  3.91 us

profile of v6, /device:TPU:1, one launch (start us, length us, event | category | flops | bytes accessed | tf_op | source)
XLA Modules:
  0.0 43.8 jit_solution(1225564633505577836)
XLA Ops:
  2.6 37.3 %grad_and_stats.1 = (f32[384,2048]{1,0:T(8,128)S(1)}, f32[384,2048]{1,0:T(8,128)S(1)}, f32[1024,768]{1,0:T(8,128)S(1)}, f32[384,2048]{1,0:T(8,128)S(1)}, f32[384...) custom-call(bf16[4096,384]{1,0:T(8,128)(2,1)} %x_hbm.1, ...), custom_call_target="tpu_custom_call" | custom-call | flops 19327352832 | bytes 60000000 | tf_op jit(solution)/shard_map/grad_and_stats/pallas_call | solution.py:308
  39.9 3.9 %apply_update.1 = (f32[384,2048]{1,0:T(8,128)}, f32[384,2048]{1,0:T(8,128)}, f32[1024,768]{1,0:T(8,128)}, f32[384]{0:T(512)}, f32[2048]{0:T(1024)}, /*index=5*/f...) custom-call(f32[384,2048]{1,0:T(8,128)S(1)} %get-tuple-element.27.g_gate, ...), custom_call_target="tpu_custom_call" | custom-call | flops 10000000 | bytes 10000000 | tf_op jit(solution)/shard_map/apply_update/pallas_call | solution.py:327
